TPU v7x, 32 devices: a whole 2x2x4 slice. The times are simulated.
32 devices in a mesh: expert: 8 (over z, y), mp: 4 (over x, core).
Axes of the slice: x: 2, y: 2, z: 4, core: 2. Of those that a mesh axis runs over, the one named last changes fastest.
Arguments:
- tokens: bfloat16 [1024, 3584], P('expert', 'mp'), may hold values from -6 to 6
- assignments: int32 [1024, 2], P('expert'), may hold values from 0 to 7, all different within a row; in each aligned block of 128 rows (0 to 127, 128 to 255, ...) at most 64 rows name the same one
- gate_probs: float32 [1024, 2], P('expert'), may hold values from 0.05 to 0.5
- expert_gate: bfloat16 [8, 3584, 2560], P('expert', None, 'mp'), may hold values from -0.09375 to 0.09375
- expert_up: bfloat16 [8, 3584, 2560], P('expert', None, 'mp'), may hold values from -0.09375 to 0.09375
- expert_down: bfloat16 [8, 2560, 3584], P('expert', 'mp'), may hold values from -0.125 to 0.125
- shared_gate: bfloat16 [3584, 10240], P('mp', 'expert'), may hold values from -0.09375 to 0.09375
- shared_up: bfloat16 [3584, 10240], P('mp', 'expert'), may hold values from -0.09375 to 0.09375
- shared_down_weight: bfloat16 [10240, 3584], P('expert', 'mp'), may hold values from -0.0625 to 0.0625
Outputs:
- layer_out: bfloat16 [1024, 3584], P('expert', 'mp')
Inputs may be any that keep to these rules, and one draw needn't show every extreme that they name: `assignments`: each row names 2 different experts; among the 128 rows of one index of the expert axis (aligned blocks) no expert is named more than 64 times.
All inputs are finite; a program needn't handle non-finite values.
Results may differ from a plain program's by a relative error of at most 0.0075.
Values may be sent and summed in bfloat16 or wider, within the bound.
No kernel may reach another device: no remote copies, remote signals or barrier semaphores. Data moves between devices by JAX's collectives and lax.ppermute only.
A program may use at most 128 MiB of HBM per device.

v0:
```python
import jax
import jax.numpy as jnp
from jax import lax
from jax.sharding import PartitionSpec as P


def split_parts(values):
    high = values.astype(jnp.bfloat16)
    low = (values - high.astype(jnp.float32)).astype(jnp.bfloat16)
    return (high, low)


def on_device(
    tokens,
    assignments,
    gate_probs,
    expert_gate,
    expert_up,
    expert_down,
    shared_gate,
    shared_up,
    shared_down_weight,
):
    experts = lax.axis_size("expert")
    local_rows, chosen = assignments.shape
    capacity = min(local_rows, max(2, 2 * local_rows * chosen // experts))
    slots_all = experts * capacity
    shared_hidden_width = shared_gate.shape[1]
    joined = jnp.concatenate([shared_gate, shared_up], axis=1)
    shared_both = jnp.dot(
        lax.all_gather(tokens, "expert", axis=0, tiled=True),
        joined,
        preferred_element_type=jnp.float32,
    )
    share = lax.psum_scatter(shared_both, "mp", scatter_dimension=0, tiled=True)
    hidden_portion_part = (
        jax.nn.silu(share[:, :shared_hidden_width]) * share[:, shared_hidden_width:]
    ).astype(jnp.bfloat16)
    shared_hidden = lax.all_gather(hidden_portion_part, "mp", axis=0, tiled=True)
    shared_result = lax.psum_scatter(
        jnp.dot(shared_hidden, shared_down_weight, preferred_element_type=jnp.float32),
        "expert",
        scatter_dimension=0,
        tiled=True,
    )
    flat_ids = assignments.reshape(-1)
    pairs = flat_ids.shape[0]
    onehot = (jnp.arange(experts, dtype=jnp.int32)[:, None] == flat_ids[None, :]).astype(jnp.int32)
    slot_rank = jnp.sum((jnp.cumsum(onehot, axis=1) - onehot) * onehot, axis=0)
    column = flat_ids * capacity + slot_rank
    picker = (column[:, None] == jnp.arange(slots_all, dtype=jnp.int32)[None, :]).astype(
        jnp.float32
    )
    owner_row = jnp.arange(pairs, dtype=jnp.int32) // chosen
    folding = (jnp.arange(local_rows, dtype=jnp.int32)[:, None] == owner_row[None, :]).astype(
        jnp.float32
    )
    indicator = jnp.dot(folding, picker, precision=lax.Precision.HIGHEST)
    dispatch = indicator.T.astype(jnp.bfloat16)
    combine = jnp.dot(
        folding, picker * gate_probs.reshape(-1)[:, None], precision=lax.Precision.HIGHEST
    )
    combine_high, combine_low = split_parts(combine)
    weight_gate = expert_gate[0]
    weight_up = expert_up[0]
    weight_down = expert_down[0]
    outgoing = jnp.dot(dispatch, tokens, preferred_element_type=jnp.float32).astype(jnp.bfloat16)
    received = lax.all_to_all(
        outgoing.reshape(experts, capacity, -1), "expert", split_axis=0, concat_axis=0, tiled=True
    )
    received = received.reshape(slots_all, -1)
    portion = lax.all_gather(received, "mp", axis=1, tiled=True)
    gate_acc = jnp.dot(portion, weight_gate, preferred_element_type=jnp.float32)
    up_acc = jnp.dot(portion, weight_up, preferred_element_type=jnp.float32)
    hidden = (jax.nn.silu(gate_acc) * up_acc).astype(jnp.bfloat16)
    partial_value = jnp.dot(hidden, weight_down, preferred_element_type=jnp.float32).astype(
        jnp.bfloat16
    )
    returned = lax.all_to_all(
        partial_value.reshape(experts, capacity, -1),
        "expert",
        split_axis=0,
        concat_axis=0,
        tiled=True,
    )
    returned = returned.reshape(slots_all, -1)
    local_sum = jnp.dot(combine_high, returned, preferred_element_type=jnp.float32) + jnp.dot(
        combine_low, returned, preferred_element_type=jnp.float32
    )
    routed = lax.psum_scatter(local_sum, "mp", scatter_dimension=1, tiled=True)
    return (shared_result + routed).astype(jnp.bfloat16)


def solution(mesh):
    in_specs = (
        P("expert", "mp"),
        P("expert", None),
        P("expert", None),
        P("expert", None, "mp"),
        P("expert", None, "mp"),
        P("expert", "mp", None),
        P("mp", "expert"),
        P("mp", "expert"),
        P("expert", "mp"),
    )
    out_specs = P("expert", "mp")
    return jax.shard_map(
        on_device, mesh=mesh, in_specs=in_specs, out_specs=out_specs, check_vma=False
    )
```

profile of v0, /device:TPU:0, one launch (start us, length us, event | category | flops | bytes accessed | tf_op | source)
XLA Modules:
  0.0 340.1 jit_solution(3035032161229359272)
XLA Ops:
  6.5 0.7 all-gather.4.cloned.1.call-update
  7.3 0.8 copy.11
  8.1 0.7 broadcast_multiply_fusion
  8.8 0.1 copy.10
  8.9 0.1 mul.44
  9.0 0.1 eq.53
  9.2 0.6 reduce-window.6
  9.8 0.2 slice_reduce_fusion
  10.1 0.4 convolution_convert_fusion.2
  10.5 1.3 convolution_convert_fusion.1
  11.8 38.0 %all_to_all.10 = bf16[8,64,896]{2,1,0:T(8,128)(2,1)} all-to-all(bf16[8,64,896]{2,1,0:T(8,128)(2,1)S(1)} %bitcast.33), channel_id=1, replica_groups=mesh['expert'=8,'mp'=4] {'expert'}, dimensions={0} | all-to-all | bytes 1835008 | tf_op jit(solution)/shard_map/all_to_all | solution.py:68
  49.9 17.3 %all-gather.4.cloned.1.call-done = bf16[1024,896]{1,0:T(8,128)(2,1)} async-done(((bf16[128,896]{1,0:T(8,128)(2,1)}), bf16[1024,896]{1,0:T(8,128)(2,1)}) %all-gather.4.cloned.1.call-update) | async-done | bytes 1835024 | tf_op jit(solution)/shard_map/all_gather | solution.py:31
  67.2 11.0 %convolution_bitcast_fusion = f32[1024,2560]{0,1:T(8,128)} fusion(bf16[1024,896]{1,0:T(8,128)(2,1)} %all-gather.4.cloned.1.call-done, bf16[896,1280]{1,0:T(8,128)(2,1)} %param.16, bf16[896,1280]{1,0:T(8,128)(2,1)} %param.15), kind=kOutput, calls=%fused_computation | convolution fusion | flops 4706795520 | bytes 16908288 | tf_op jit(solution)/shard_map/dot_general | solution.py:30
  78.2 20.7 %all-gather.8.cloned.1.call-done = bf16[512,3584]{1,0:T(8,128)(2,1)} async-done(((bf16[512,896]{1,0:T(8,128)(2,1)}), bf16[512,3584]{1,0:T(8,128)(2,1)}) %all-gather.8.cloned.1.call-update) | async-done | bytes 3670032 | tf_op jit(solution)/shard_map/all_gather | solution.py:72
  99.0 6.5 %fusion.6 = f32[512,640]{1,0:T(8,128)S(1)} fusion(bf16[512,3584]{1,0:T(8,128)(2,1)} %all-gather.8.cloned.1.call-done, bf16[1,3584,640]{2,1,0:T(8,128)(2,1)} %param.12), kind=kOutput, calls=%fused_computation.9 | convolution fusion | flops 2348810240 | bytes 9568256 | tf_op jit(solution)/shard_map/dot_general | solution.py:73
  105.5 6.2 %fusion.11 = bf16[512,640]{1,0:T(8,128)(2,1)S(1)} fusion(bf16[512,3584]{1,0:T(8,128)(2,1)S(1)} %copy-done.2, bf16[1,3584,640]{2,1,0:T(8,128)(2,1)} %param.13, f32[512,640]{1,0:T(8,128)S(1)} %fusion.6), kind=kOutput, calls=%fused_computation.13 | convolution fusion | flops 2350776320 | bytes 10223616 | tf_op jit(solution)/shard_map/dot_general | solution.py:74
  111.7 8.3 %convolution_convert_fusion = bf16[512,3584]{1,0:T(8,128)(2,1)} fusion(bf16[512,640]{1,0:T(8,128)(2,1)S(1)} %fusion.11, bf16[1,640,3584]{2,1,0:T(8,128)(2,1)} %param.14), kind=kOutput, calls=%fused_computation.1 | convolution fusion | flops 2350645248 | bytes 8912896 | tf_op jit(solution)/shard_map/dot_general | solution.py:76
  120.0 5.2 %all-to-all-start.1 = ((bf16[8,64,3584]{2,1,0:T(8,128)(2,1)}), bf16[8,64,3584]{2,1,0:T(8,128)(2,1)}, u32[]{:S(2)}, u32[]{:S(2)}) async-start(bf16[8,64,3584]{2,1,0:T(8,128)(2,1)} %bitcast.31), calls=%async_computation.3 | async-start | bytes 7340032 | tf_op jit(solution)/shard_map/all_to_all | solution.py:79
  125.3 60.5 %reduce-scatter.4.cloned.1.call-done = f32[256,2560]{0,1:T(8,128)} async-done(((f32[1024,2560]{0,1:T(8,128)}), f32[256,2560]{0,1:T(8,128)}) %reduce-scatter.4.cloned.1.call-update) | async-done | bytes 2621456 | tf_op jit(solution)/shard_map/reduce_scatter | solution.py:35
  185.8 3.0 fusion.14
  188.8 0.2 reduce-scatter.8.cloned.1.call-start
  189.0 0.1 copy.12
  189.2 0.1 mul.46
  189.3 0.5 fusion.15
  189.8 18.0 %all-to-all-done.1 = bf16[8,64,3584]{2,1,0:T(8,128)(2,1)} async-done(((bf16[8,64,3584]{2,1,0:T(8,128)(2,1)}), bf16[8,64,3584]{2,1,0:T(8,128)(2,1)}, u32[]{:S(2)}, u32[]{:S(2)}) %all-to-all-start.1) | async-done | bytes 3670048 | tf_op jit(solution)/shard_map/all_to_all | solution.py:79
  207.8 2.7 fusion.24
  210.5 4.0 %convolution_add_fusion = f32[128,3584]{1,0:T(8,128)} fusion(f32[128,3584]{1,0:T(8,128)S(1)} %fusion.24, bf16[512,3584]{1,0:T(8,128)(2,1)} %bitcast.8, f32[128,512]{1,0:T(8,128)S(1)} %fusion.15), kind=kOutput, calls=%fused_computation.2 | convolution fusion | flops 470482944 | bytes 7602176 | tf_op jit(solution)/shard_map/dot_general | solution.py:87
  214.6 0.3 all-gather.6.cloned.1.call-done
  214.9 6.5 %fusion.31 = f32[1024,896]{1,0:T(8,128)} fusion(bf16[1024,1280]{0,1:T(8,128)(2,1)} %all-gather.6.cloned.1.call-done, bf16[1280,896]{1,0:T(8,128)(2,1)S(1)} %copy-done), kind=kOutput, calls=%fused_computation.45 | convolution fusion | flops 2348810240 | bytes 8585216 | tf_op jit(solution)/shard_map/dot_general | solution.py:41
  221.3 25.5 %reduce-scatter.8.cloned.1.call-done = f32[128,896]{1,0:T(8,128)} async-done(((f32[128,3584]{1,0:T(8,128)}), f32[128,896]{1,0:T(8,128)}) %reduce-scatter.8.cloned.1.call-update) | async-done | bytes 458768 | tf_op jit(solution)/shard_map/reduce_scatter | solution.py:90
  246.9 84.5 %reduce-scatter.6.cloned.1.call-done = f32[128,896]{1,0:T(8,128)} async-done(((f32[1024,896]{1,0:T(8,128)}), f32[128,896]{1,0:T(8,128)}) %reduce-scatter.6.cloned.1.call-update) | async-done | bytes 458768 | tf_op jit(solution)/shard_map/reduce_scatter | solution.py:40
  331.3 1.9 add_convert_fusion
  (21 shorter events, 0.4 us)
Async XLA Ops:
  6.5 208.3 %copy-start = (bf16[1280,896]{1,0:T(8,128)(2,1)S(1)}, bf16[1280,896]{1,0:T(8,128)(2,1)}, u32[]{:S(2)}) copy-start(bf16[1280,896]{1,0:T(8,128)(2,1)} %param.17) | copy-start | bytes 6881284
  6.5 60.7 %all-gather.4.cloned.1.call-start = ((), (), s32[]{:S(2)}) async-start(), calls=%async_computation.5 | async-start | bytes 2064384 | tf_op jit(solution)/shard_map/all_gather | solution.py:31
  7.3 91.7 %all-gather.8.cloned.1.call-start = ((), (), s32[]{:S(2)}) async-start(), calls=%async_computation.9 | async-start | bytes 4587520 | tf_op jit(solution)/shard_map/all_gather | solution.py:72
  49.8 136.0 %reduce-scatter.4.cloned.1.call-start = ((), (), s32[]{:S(2)}) async-start(), calls=%async_computation.6 | async-start | bytes 13107200 | tf_op jit(solution)/shard_map/reduce_scatter | solution.py:35
  99.0 6.6 %copy-start.2 = (bf16[512,3584]{1,0:T(8,128)(2,1)S(1)}, bf16[512,3584]{1,0:T(8,128)(2,1)}, u32[]{:S(2)}) copy-start(bf16[512,3584]{1,0:T(8,128)(2,1)} %all-gather.8.cloned.1.call-done) | copy-start | bytes 11010052
  120.0 87.8 %all-to-all-start.1 = ((bf16[8,64,3584]{2,1,0:T(8,128)(2,1)}), bf16[8,64,3584]{2,1,0:T(8,128)(2,1)}, u32[]{:S(2)}, u32[]{:S(2)}) async-start(bf16[8,64,3584]{2,1,0:T(8,128)(2,1)} %bitcast.31), calls=%async_computation.3 | async-start | bytes 7340032 | tf_op jit(solution)/shard_map/all_to_all | solution.py:79
  125.2 63.8 %copy-start.1 = (f32[128,2]{0,1:T(2,128)S(1)}, f32[128,2]{0,1:T(2,128)}, u32[]{:S(2)}) copy-start(f32[128,2]{0,1:T(2,128)} %param.11) | copy-start | bytes 3076
  125.2 89.6 %all-gather.6.cloned.1.call-start = ((), (), s32[]{:S(2)}) async-start(), calls=%async_computation.7 | async-start | bytes 3276800 | tf_op jit(solution)/shard_map/all_gather | solution.py:39
  188.8 58.1 %reduce-scatter.8.cloned.1.call-start = ((), (), s32[]{:S(2)}) async-start(), calls=%async_computation.10 | async-start | bytes 2293760 | tf_op jit(solution)/shard_map/reduce_scatter | solution.py:90
  214.5 116.8 %reduce-scatter.6.cloned.1.call-start = ((), (), s32[]{:S(2)}) async-start(), calls=%async_computation.8 | async-start | bytes 4128768 | tf_op jit(solution)/shard_map/reduce_scatter | solution.py:40
Sparse Core Ops, SparseCore 0:
  9.5 57.6 all-gather.3
  68.8 30.1 all-gather.7
  101.6 84.1 reduce-scatter.3
  188.9 25.8 all-gather.5
  217.2 29.5 reduce-scatter.7
  250.4 80.9 reduce-scatter.5
where the time goes:
time: 341 us; the launch traced here: 340 us
  waiting for transfers between devices  228 us (67%)
  matrix products  47.3 us (14%)
  blocking collectives  38 us (11%)
  between operations  13.6 us (4%)
  other arithmetic  6.28 us (2%)
  starting transfers between devices  5.61 us (2%)
    reduce_scatter x1, waiting for transfers between devices, on_device(): lax.psum_scatter(jnp.dot(shared_hidden, shared_down_weight, preferred_ele...  84.5 us
    reduce_scatter x1, waiting for transfers between devices, on_device(): share = lax.psum_scatter(shared_both, 'mp', scatter_dimension=0, tiled=True)  60.5 us
    all_to_all x1, blocking collectives, on_device(): lax.all_to_all(outgoing.reshape(experts, capacity, -1), 'expert', split_a...  38 us
    reduce_scatter x1, waiting for transfers between devices, on_device(): routed = lax.psum_scatter(local_sum, 'mp', scatter_dimension=1, tiled=True)  25.5 us
    all_gather x1, waiting for transfers between devices, on_device(): portion = lax.all_gather(received, 'mp', axis=1, tiled=True)  20.7 us
    all_to_all x1, waiting for transfers between devices, on_device(): lax.all_to_all(partial_value.reshape(experts, capacity, -1), 'expert', sp...  18 us
    all_gather x1, waiting for transfers between devices, on_device(): lax.all_gather(tokens, 'expert', axis=0, tiled=True)  17.3 us
    dot_general x1, matrix products, on_device(): jnp.dot(lax.all_gather(tokens, 'expert', axis=0, tiled=True), joined, pre...  11 us
  transfers between devices with their start and end apart: 7, of which 7 were waited for; matrix products, arithmetic and copies ran while one was open for 16% of the time, Pallas kernels for 0%

commit v1 on v0

--- a/solution.py
+++ b/solution.py
@@ -2,6 +2,17 @@
 import jax.numpy as jnp
 from jax import lax
 from jax.sharding import PartitionSpec as P
+
+
+def cut_along(x, dim, size):
+    before, after = (x.shape[:dim], x.shape[dim + 1 :])
+    return jnp.moveaxis(x.reshape(*before, size, -1, *after), dim, 0)
+
+
+def laid_out(pieces, dim):
+    pieces = jnp.moveaxis(pieces, 0, dim)
+    shape = pieces.shape
+    return pieces.reshape(*shape[:dim], shape[dim] * shape[dim + 1], *shape[dim + 2 :])
 
 
 def split_parts(values):
@@ -65,9 +76,16 @@
     weight_up = expert_up[0]
     weight_down = expert_down[0]
     outgoing = jnp.dot(dispatch, tokens, preferred_element_type=jnp.float32).astype(jnp.bfloat16)
-    received = lax.all_to_all(
-        outgoing.reshape(experts, capacity, -1), "expert", split_axis=0, concat_axis=0, tiled=True
-    )
+    x = outgoing.reshape(experts, capacity, -1)
+    size, position = (lax.axis_size("expert"), lax.axis_index("expert"))
+    parts = cut_along(x, 0, size)
+    whole = parts
+    for step in range(1, size):
+        target, source = ((position + step) % size, (position - step) % size)
+        sent = lax.dynamic_index_in_dim(parts, target, 0)
+        theirs = lax.ppermute(sent, "expert", [(i, (i + step) % size) for i in range(size)])
+        whole = lax.dynamic_update_slice_in_dim(whole, theirs, source, axis=0)
+    received = laid_out(whole, 0)
     received = received.reshape(slots_all, -1)
     portion = lax.all_gather(received, "mp", axis=1, tiled=True)
     gate_acc = jnp.dot(portion, weight_gate, preferred_element_type=jnp.float32)

time: 341 us -> 343 us (level)
  blocking collectives: 38 us -> 0 us
  waiting for transfers between devices: 228 us -> 258 us
  starting transfers between devices: 5.61 us -> 16.7 us
  matrix products: 47.3 us -> 43.8 us
    all_to_all x1 -> x0, blocking collectives: 38 us -> none  [on_device(): lax.all_to_all(outgoing.reshape(experts, capacity, -1), 'expert', split_a...]
    ppermute x0 -> x7, waiting for transfers between devices: none -> 20.1 us  [on_device(): lax.ppermute(sent, 'expert', [(i, (i + step) % size) for i in range(size)])]
    ppermute x0 -> x7, starting transfers between devices: none -> 11 us  [on_device(): lax.ppermute(sent, 'expert', [(i, (i + step) % size) for i in range(size)])]
    all_gather x1, waiting for transfers between devices: 17.3 us -> 24.6 us  [on_device(): lax.all_gather(tokens, 'expert', axis=0, tiled=True)]
    dot_general x1, matrix products: 8.27 us -> 4.82 us  [on_device(): jnp.dot(hidden, weight_down, preferred_element_type=jnp.float32)]
  transfers between devices with their start and end apart: 7 -> 14, of which waited for: 7 -> 11; matrix products, arithmetic and copies ran while one was open for 16% -> 15% of each run, Pallas kernels for 0% -> 0%
where the time goes in v1:
time: 343 us
  waiting for transfers between devices  258 us (75%)
  matrix products  43.8 us (13%)
  starting transfers between devices  16.7 us (5%)
  between operations  13.7 us (4%)
  other arithmetic  6.26 us (2%)
  local copies, waits for them, and re-layouts  4.1 us (1%)
    reduce_scatter x1, waiting for transfers between devices, on_device(): lax.psum_scatter(jnp.dot(shared_hidden, shared_down_weight, preferred_ele...  84.4 us
    reduce_scatter x1, waiting for transfers between devices, on_device(): share = lax.psum_scatter(shared_both, 'mp', scatter_dimension=0, tiled=True)  63.8 us
    reduce_scatter x1, waiting for transfers between devices, on_device(): routed = lax.psum_scatter(local_sum, 'mp', scatter_dimension=1, tiled=True)  25.5 us
    all_gather x1, waiting for transfers between devices, on_device(): lax.all_gather(tokens, 'expert', axis=0, tiled=True)  24.6 us
    all_gather x1, waiting for transfers between devices, on_device(): portion = lax.all_gather(received, 'mp', axis=1, tiled=True)  20.8 us
    ppermute x7, waiting for transfers between devices, on_device(): lax.ppermute(sent, 'expert', [(i, (i + step) % size) for i in range(size)])  20.1 us
    all_to_all x1, waiting for transfers between devices, on_device(): lax.all_to_all(partial_value.reshape(experts, capacity, -1), 'expert', sp...  14.7 us
    ppermute x7, starting transfers between devices, on_device(): lax.ppermute(sent, 'expert', [(i, (i + step) % size) for i in range(size)])  11 us
  transfers between devices with their start and end apart: 14, of which 11 were waited for; matrix products, arithmetic and copies ran while one was open for 15% of the time, Pallas kernels for 0%

profile of v1, /device:TPU:0, one launch (start us, length us, event | category | flops | bytes accessed | tf_op | source)
XLA Modules:
  0.0 342.8 jit_solution(18373507152985194445)
XLA Ops:
  6.5 0.7 all-gather.4.cloned.1.call-update
  7.3 0.8 copy.11
  8.1 0.7 broadcast_multiply_fusion
  11.1 1.3 convolution_convert_fusion.1
  12.5 3.1 collective-permute-start
  15.5 6.2 %collective-permute-done = bf16[1,1,64,896]{3,2,0,1:T(8,128)(2,1)S(1)} collective-permute-done((bf16[1,1,64,896]{3,2,0,1:T(8,128)(2,1)S(1)}, bf16[1,1,64,896]{3,2,0,1:T(8,128)(2,1)S(1)}, u32[]{:S(2)}, u32[]{:S(2)}) %collective-permute-start) | collective-permute-done | bytes 114720 | tf_op jit(solution)/shard_map/ppermute | solution.py:86
  21.7 0.8 constant_dynamic-slice_fusion
  22.5 1.3 collective-permute-start.2
  23.8 1.2 collective-permute-start.3
  25.0 3.5 %collective-permute-start.4 = (bf16[1,1,64,896]{3,2,0,1:T(8,128)(2,1)}, bf16[1,1,64,896]{3,2,0,1:T(8,128)(2,1)S(1)}, u32[]{:S(2)}, u32[]{:S(2)}) collective-permute-start(bf16[1,1,64,896]{3,2,0,1:T(8,128)(2,1)} %get-tuple-element.7), channel_id=1, source_target_pairs={{0,20},{4,24},{8,28},{12,0},{16,4},{20,8},{24,12},{28,16},{1,21},{... | collective-permute-start | bytes 344072 | tf_op jit(solution)/shard_map/ppermute | solution.py:86
  28.5 1.6 collective-permute-start.5
  30.1 2.3 collective-permute-done.1
  32.8 8.1 %collective-permute-done.2 = bf16[1,1,64,896]{3,2,0,1:T(8,128)(2,1)S(1)} collective-permute-done((bf16[1,1,64,896]{3,2,0,1:T(8,128)(2,1)}, bf16[1,1,64,896]{3,2,0,1:T(8,128)(2,1)S(1)}, u32[]{:S(2)}, u32[]{:S(2)}) %collective-permute-start.2) | collective-permute-done | bytes 114720 | tf_op jit(solution)/shard_map/ppermute | solution.py:86
  40.9 3.4 %collective-permute-done.3 = bf16[1,1,64,896]{3,2,0,1:T(8,128)(2,1)S(1)} collective-permute-done((bf16[1,1,64,896]{3,2,0,1:T(8,128)(2,1)}, bf16[1,1,64,896]{3,2,0,1:T(8,128)(2,1)S(1)}, u32[]{:S(2)}, u32[]{:S(2)}) %collective-permute-start.3) | collective-permute-done | bytes 114720 | tf_op jit(solution)/shard_map/ppermute | solution.py:86
  44.5 0.9 copy-done.1
  45.5 24.6 %all-gather.4.cloned.1.call-done = bf16[1024,896]{1,0:T(8,128)(2,1)} async-done(((bf16[128,896]{1,0:T(8,128)(2,1)}), bf16[1024,896]{1,0:T(8,128)(2,1)}) %all-gather.4.cloned.1.call-update) | async-done | bytes 1835024 | tf_op jit(solution)/shard_map/all_gather | solution.py:42
  70.0 10.9 %convolution_bitcast_fusion = f32[1024,2560]{0,1:T(8,128)} fusion(bf16[1024,896]{1,0:T(8,128)(2,1)} %all-gather.4.cloned.1.call-done, bf16[896,1280]{1,0:T(8,128)(2,1)} %param.16, bf16[896,1280]{1,0:T(8,128)(2,1)} %param.15), kind=kOutput, calls=%fused_computation | convolution fusion | flops 4706795520 | bytes 16908288 | tf_op jit(solution)/shard_map/dot_general | solution.py:41
  81.0 20.8 %all-gather.8.cloned.1.call-done = bf16[512,3584]{1,0:T(8,128)(2,1)} async-done(((bf16[512,896]{1,0:T(8,128)(2,1)}), bf16[512,3584]{1,0:T(8,128)(2,1)}) %all-gather.8.cloned.1.call-update) | async-done | bytes 3670032 | tf_op jit(solution)/shard_map/all_gather | solution.py:90
  101.8 6.5 %fusion.4 = f32[512,640]{1,0:T(8,128)S(1)} fusion(bf16[512,3584]{1,0:T(8,128)(2,1)} %all-gather.8.cloned.1.call-done, bf16[1,3584,640]{2,1,0:T(8,128)(2,1)} %param.13), kind=kOutput, calls=%fused_computation.7 | convolution fusion | flops 2348810240 | bytes 9568256 | tf_op jit(solution)/shard_map/dot_general | solution.py:92
  108.4 6.2 %fusion.6 = f32[512,640]{1,0:T(8,128)S(1)} fusion(bf16[512,3584]{1,0:T(8,128)(2,1)S(1)} %copy-done.7, bf16[1,3584,640]{2,1,0:T(8,128)(2,1)} %param.12), kind=kOutput, calls=%fused_computation.9 | convolution fusion | flops 2348810240 | bytes 9568256 | tf_op jit(solution)/shard_map/dot_general | solution.py:91
  114.6 4.8 %convolution_convert_fusion = bf16[512,3584]{1,0:T(8,128)(2,1)} fusion(bf16[1,640,3584]{2,1,0:T(8,128)(2,1)S(1)} %bitcast.31, f32[512,640]{1,0:T(8,128)S(1)} %fusion.4, f32[512,640]{1,0:T(8,128)S(1)} %fusion.6), kind=kOutput, calls=%fused_computation.1 | convolution fusion | flops 2352611328 | bytes 10878976 | tf_op jit(solution)/shard_map/dot_general | solution.py:94
  119.5 5.3 %all-to-all-start = ((bf16[8,64,3584]{2,1,0:T(8,128)(2,1)}), bf16[8,64,3584]{2,1,0:T(8,128)(2,1)}, u32[]{:S(2)}, u32[]{:S(2)}) async-start(bf16[8,64,3584]{2,1,0:T(8,128)(2,1)} %bitcast.29), calls=%async_computation.2 | async-start | bytes 7340032 | tf_op jit(solution)/shard_map/all_to_all | solution.py:97
  124.8 63.8 %reduce-scatter.4.cloned.1.call-done = f32[256,2560]{0,1:T(8,128)} async-done(((f32[1024,2560]{0,1:T(8,128)}), f32[256,2560]{0,1:T(8,128)}) %reduce-scatter.4.cloned.1.call-update) | async-done | bytes 2621456 | tf_op jit(solution)/shard_map/reduce_scatter | solution.py:46
  188.7 3.0 fusion.8
  192.6 14.7 %all-to-all-done = bf16[8,64,3584]{2,1,0:T(8,128)(2,1)} async-done(((bf16[8,64,3584]{2,1,0:T(8,128)(2,1)}), bf16[8,64,3584]{2,1,0:T(8,128)(2,1)}, u32[]{:S(2)}, u32[]{:S(2)}) %all-to-all-start) | async-done | bytes 3670048 | tf_op jit(solution)/shard_map/all_to_all | solution.py:97
  207.3 2.7 fusion.19
  210.0 4.0 %convolution_add_fusion = f32[128,3584]{1,0:T(8,128)} fusion(f32[128,3584]{1,0:T(8,128)S(1)} %fusion.19, bf16[512,3584]{1,0:T(8,128)(2,1)} %bitcast.8, f32[128,512]{1,0:T(8,128)S(1)} %fusion.10), kind=kOutput, calls=%fused_computation.2 | convolution fusion | flops 470482944 | bytes 7602176 | tf_op jit(solution)/shard_map/dot_general | solution.py:105
  214.1 3.6 %all-gather.6.cloned.1.call-done = bf16[1024,1280]{0,1:T(8,128)(2,1)} async-done(((bf16[256,1280]{0,1:T(8,128)(2,1)}), bf16[1024,1280]{0,1:T(8,128)(2,1)}) %all-gather.6.cloned.1.call-update) | async-done | bytes 2621456 | tf_op jit(solution)/shard_map/all_gather | solution.py:50
  217.7 6.4 %fusion.27 = f32[1024,896]{1,0:T(8,128)} fusion(bf16[1024,1280]{0,1:T(8,128)(2,1)} %all-gather.6.cloned.1.call-done, bf16[1280,896]{1,0:T(8,128)(2,1)S(1)} %copy-done), kind=kOutput, calls=%fused_computation.60 | convolution fusion | flops 2348810240 | bytes 8585216 | tf_op jit(solution)/shard_map/dot_general | solution.py:52
  224.1 25.5 %reduce-scatter.8.cloned.1.call-done = f32[128,896]{1,0:T(8,128)} async-done(((f32[128,3584]{1,0:T(8,128)}), f32[128,896]{1,0:T(8,128)}) %reduce-scatter.8.cloned.1.call-update) | async-done | bytes 458768 | tf_op jit(solution)/shard_map/reduce_scatter | solution.py:108
  249.7 84.4 %reduce-scatter.6.cloned.1.call-done = f32[128,896]{1,0:T(8,128)} async-done(((f32[1024,896]{1,0:T(8,128)}), f32[128,896]{1,0:T(8,128)}) %reduce-scatter.6.cloned.1.call-update) | async-done | bytes 458768 | tf_op jit(solution)/shard_map/reduce_scatter | solution.py:51
  334.1 1.9 add_convert_fusion
  (57 shorter events, 3.9 us)
Async XLA Ops:
  6.5 211.1 %copy-start = (bf16[1280,896]{1,0:T(8,128)(2,1)S(1)}, bf16[1280,896]{1,0:T(8,128)(2,1)}, u32[]{:S(2)}) copy-start(bf16[1280,896]{1,0:T(8,128)(2,1)} %param.17) | copy-start | bytes 6881284
  6.5 63.5 %all-gather.4.cloned.1.call-start = ((), (), s32[]{:S(2)}) async-start(), calls=%async_computation.4 | async-start | bytes 2064384 | tf_op jit(solution)/shard_map/all_gather | solution.py:42
  7.3 94.6 %all-gather.8.cloned.1.call-start = ((), (), s32[]{:S(2)}) async-start(), calls=%async_computation.8 | async-start | bytes 4587520 | tf_op jit(solution)/shard_map/all_gather | solution.py:90
  10.2 0.6 copy-start.3
  10.2 0.6 copy-start.5
  12.5 9.2 %collective-permute-start = (bf16[1,1,64,896]{3,2,0,1:T(8,128)(2,1)S(1)}, bf16[1,1,64,896]{3,2,0,1:T(8,128)(2,1)S(1)}, u32[]{:S(2)}, u32[]{:S(2)}) collective-permute-start(bf16[1,1,64,896]{3,2,0,1:T(8,128)(2,1)S(1)} %constant_dynamic-slice_fusion.6), channel_id=1, source_target_pairs={{0,4},{4,8},{8,12},{12,16},{16,20},{20,24},{24,28},{28,0},{1,5},{5... | collective-permute-start | bytes 344072 | tf_op jit(solution)/shard_map/ppermute | solution.py:86
  22.5 10.0 %collective-permute-start.1 = (bf16[1,1,64,896]{3,2,0,1:T(8,128)(2,1)}, bf16[1,1,64,896]{3,2,0,1:T(8,128)(2,1)S(1)}, u32[]{:S(2)}, u32[]{:S(2)}) collective-permute-start(bf16[1,1,64,896]{3,2,0,1:T(8,128)(2,1)} %get-tuple-element.10), channel_id=1, source_target_pairs={{0,8},{4,12},{8,16},{12,20},{16,24},{20,28},{24,0},{28,4},{1,9},{5... | collective-permute-start | bytes 344072 | tf_op jit(solution)/shard_map/ppermute | solution.py:86
  22.5 18.4 %collective-permute-start.2 = (bf16[1,1,64,896]{3,2,0,1:T(8,128)(2,1)}, bf16[1,1,64,896]{3,2,0,1:T(8,128)(2,1)S(1)}, u32[]{:S(2)}, u32[]{:S(2)}) collective-permute-start(bf16[1,1,64,896]{3,2,0,1:T(8,128)(2,1)} %get-tuple-element.9), channel_id=1, source_target_pairs={{0,12},{4,16},{8,20},{12,24},{16,28},{20,0},{24,4},{28,8},{1,13},{... | collective-permute-start | bytes 344072 | tf_op jit(solution)/shard_map/ppermute | solution.py:86
  23.8 20.6 %collective-permute-start.3 = (bf16[1,1,64,896]{3,2,0,1:T(8,128)(2,1)}, bf16[1,1,64,896]{3,2,0,1:T(8,128)(2,1)S(1)}, u32[]{:S(2)}, u32[]{:S(2)}) collective-permute-start(bf16[1,1,64,896]{3,2,0,1:T(8,128)(2,1)} %get-tuple-element.8), channel_id=1, source_target_pairs={{0,16},{4,20},{8,24},{12,28},{16,0},{20,4},{24,8},{28,12},{1,17},{... | collective-permute-start | bytes 344072 | tf_op jit(solution)/shard_map/ppermute | solution.py:86
  25.0 19.4 %collective-permute-start.4 = (bf16[1,1,64,896]{3,2,0,1:T(8,128)(2,1)}, bf16[1,1,64,896]{3,2,0,1:T(8,128)(2,1)S(1)}, u32[]{:S(2)}, u32[]{:S(2)}) collective-permute-start(bf16[1,1,64,896]{3,2,0,1:T(8,128)(2,1)} %get-tuple-element.7), channel_id=1, source_target_pairs={{0,20},{4,24},{8,28},{12,0},{16,4},{20,8},{24,12},{28,16},{1,21},{... | collective-permute-start | bytes 344072 | tf_op jit(solution)/shard_map/ppermute | solution.py:86
  28.5 15.8 %collective-permute-start.5 = (bf16[1,1,64,896]{3,2,0,1:T(8,128)(2,1)S(1)}, bf16[1,1,64,896]{3,2,0,1:T(8,128)(2,1)S(1)}, u32[]{:S(2)}, u32[]{:S(2)}) collective-permute-start(bf16[1,1,64,896]{3,2,0,1:T(8,128)(2,1)S(1)} %get-tuple-element.6), channel_id=1, source_target_pairs={{0,24},{4,28},{8,0},{12,4},{16,8},{20,12},{24,16},{28,20},{1,25},{... | collective-permute-start | bytes 344072 | tf_op jit(solution)/shard_map/ppermute | solution.py:86
  32.5 12.0 %collective-permute-start.6 = (bf16[1,1,64,896]{3,2,0,1:T(8,128)(2,1)S(1)}, bf16[1,1,64,896]{3,2,0,1:T(8,128)(2,1)S(1)}, u32[]{:S(2)}, u32[]{:S(2)}) collective-permute-start(bf16[1,1,64,896]{3,2,0,1:T(8,128)(2,1)S(1)} %get-tuple-element.5), channel_id=1, source_target_pairs={{0,28},{4,0},{8,4},{12,8},{16,12},{20,16},{24,20},{28,24},{1,29},{... | collective-permute-start | bytes 344072 | tf_op jit(solution)/shard_map/ppermute | solution.py:86
  44.5 0.9 copy-start.1
  45.4 143.2 %reduce-scatter.4.cloned.1.call-start = ((), (), s32[]{:S(2)}) async-start(), calls=%async_computation.5 | async-start | bytes 13107200 | tf_op jit(solution)/shard_map/reduce_scatter | solution.py:46
  101.8 6.6 %copy-start.7 = (bf16[512,3584]{1,0:T(8,128)(2,1)S(1)}, bf16[512,3584]{1,0:T(8,128)(2,1)}, u32[]{:S(2)}) copy-start(bf16[512,3584]{1,0:T(8,128)(2,1)} %all-gather.8.cloned.1.call-done) | copy-start | bytes 11010052
  101.8 12.8 %slice-start = ((s8[4587520]{0:T(1024)(128)(4,1)}), s8[4194304]{0:T(1024)(128)(4,1)S(1)}, s32[]{:S(2)}) async-start(s8[4587520]{0:T(1024)(128)(4,1)} %bitcast.30), calls=%async_computation.10 | async-start | bytes 8388608
  108.4 6.2 %slice-start.1 = ((s8[4587520]{0:T(1024)(128)(4,1)}), s8[393216]{0:T(1024)(128)(4,1)S(1)}, s32[]{:S(2)}) async-start(s8[4587520]{0:T(1024)(128)(4,1)} %bitcast.30), calls=%async_computation.11 | async-start | bytes 786432
  119.5 87.9 %all-to-all-start = ((bf16[8,64,3584]{2,1,0:T(8,128)(2,1)}), bf16[8,64,3584]{2,1,0:T(8,128)(2,1)}, u32[]{:S(2)}, u32[]{:S(2)}) async-start(bf16[8,64,3584]{2,1,0:T(8,128)(2,1)} %bitcast.29), calls=%async_computation.2 | async-start | bytes 7340032 | tf_op jit(solution)/shard_map/all_to_all | solution.py:97
  124.8 67.1 %copy-start.2 = (f32[128,2]{0,1:T(2,128)S(1)}, f32[128,2]{0,1:T(2,128)}, u32[]{:S(2)}) copy-start(f32[128,2]{0,1:T(2,128)} %param.11) | copy-start | bytes 3076
  124.8 67.4 %copy-start.4 = (s32[256]{0:T(256)S(1)}, s32[256]{0:T(256)}, u32[]{:S(2)}) copy-start(s32[256]{0:T(256)} %copy-done.3) | copy-start | bytes 3076
  124.8 67.4 %copy-start.6 = (s32[256]{0:T(256)S(1)}, s32[256]{0:T(256)}, u32[]{:S(2)}) copy-start(s32[256]{0:T(256)} %copy-done.5) | copy-start | bytes 3076
  124.8 92.9 %all-gather.6.cloned.1.call-start = ((), (), s32[]{:S(2)}) async-start(), calls=%async_computation.6 | async-start | bytes 3276800 | tf_op jit(solution)/shard_map/all_gather | solution.py:50
  191.6 58.0 %reduce-scatter.8.cloned.1.call-start = ((), (), s32[]{:S(2)}) async-start(), calls=%async_computation.9 | async-start | bytes 2293760 | tf_op jit(solution)/shard_map/reduce_scatter | solution.py:108
  214.0 120.0 %reduce-scatter.6.cloned.1.call-start = ((), (), s32[]{:S(2)}) async-start(), calls=%async_computation.7 | async-start | bytes 4128768 | tf_op jit(solution)/shard_map/reduce_scatter | solution.py:51
Sparse Core Ops, SparseCore 0:
  9.5 60.4 all-gather.3
  71.6 30.1 all-gather.7
  104.4 84.1 reduce-scatter.3
  191.8 25.8 all-gather.5
  220.0 29.5 reduce-scatter.7
  253.2 80.8 reduce-scatter.5
